TPU v7x, 512 devices: a whole 4x8x8 slice. The times are simulated.
512 devices in a mesh: dp: 64 (over z, y), tm: 8 (over x, core).
Axes of the slice: x: 4, y: 8, z: 8, core: 2. Of those that a mesh axis runs over, the one named last changes fastest.
Arguments:
- hidden: bfloat16 [128, 1024, 4096], P('dp', 'tm'), may hold values from -6 to 6
- first_weight: bfloat16 [4096, 1024], P('dp'), may hold values from -0.09375 to 0.09375
- first_bias: float32 [1024], replicated, may hold values from -3 to 3
- second_weight: float32 [1024], replicated, may hold values from -0.1875 to 0.1875
- second_bias: float32 [1], replicated, may hold values from -3 to 3
- rewards: float32 [128, 1024], P('dp', 'tm'), may hold values from -0.8 to 0.8
- dones: int32 [128, 1024], P('dp', 'tm'), may hold values 0 or 1
- lengths: int32 [128], P('dp'), may hold values from 512 to 1024
- discount: float32 [128], P('dp'), may hold values from 0.96 to 1
- trace: float32 [128], P('dp'), may hold values from 0.99902344 to 1
Outputs:
- advantages: float32 [128, 1024], P('dp', 'tm')
- returns: float32 [128, 1024], P('dp', 'tm')
All inputs are finite; a program needn't handle non-finite values. No bound on the sum of `dones` on one device may be relied on, other than what follows from the above.
Results may differ from a plain program's by a relative error of at most 0.0003.
Values may be sent and summed in bfloat16 or wider, within the bound.
A program may use at most 64 MiB of HBM per device.

v0:
```python
import functools

import jax
import jax.numpy as jnp
from jax import lax
from jax.sharding import Mesh
from jax.sharding import PartitionSpec as P

DP = ("dp_0", "dp_1")
TM = ("tm_0", "tm_1")
DP_TM = ("dp_0", "dp_1", "tm_0", "tm_1")


def passed_along(block, axis, distance):
    devices = range(lax.axis_size(axis))
    route = [(i - distance, i) for i in devices if i - distance in devices]
    return lax.ppermute(block, axis, route)


def sent_together(arrays, axis, dim, along):
    both = jnp.concatenate(arrays, axis=along)
    whole, at, outs = (lax.all_gather(both, axis, axis=dim, tiled=True), 0, [])
    for a in arrays:
        outs.append(lax.slice_in_dim(whole, at, at + a.shape[along], axis=along))
        at += a.shape[along]
    return tuple(outs)


def one_axis_at_a_time(array, axes):
    return functools.reduce(lax.psum, axes, array)


def pair_combine(earlier, later):
    return (earlier[0] * later[0], later[1] + later[0] * earlier[1])


def local_suffix(decay, delta):
    return lax.associative_scan(pair_combine, (decay, delta), reverse=True, axis=1)


def on_device(
    hidden,
    first_weight,
    first_bias,
    second_weight,
    second_bias,
    rewards,
    dones,
    lengths,
    discount,
    trace,
):
    traj_local, step_local, feature_count = hidden.shape
    row_count = traj_local * step_local
    token_rows = hidden.reshape(row_count, feature_count)
    whole_weight = lax.all_gather(first_weight, DP, axis=0, tiled=True)
    pre = jnp.dot(token_rows, whole_weight, preferred_element_type=jnp.float32)
    values = jnp.dot(jax.nn.silu(pre + first_bias), second_weight, precision=lax.Precision.HIGHEST)
    values = (values + second_bias[0]).reshape(traj_local, step_local)
    time_index = lax.axis_index(TM) * step_local + jnp.arange(step_local, dtype=jnp.int32)
    live = (time_index[None, :] < lengths[:, None]).astype(jnp.float32)
    live_next = ((time_index + 1)[None, :] < lengths[:, None]).astype(jnp.float32)
    keep = 1.0 - dones.astype(jnp.float32)
    following = passed_along(values[:, :1], TM, -1)
    value_next = jnp.concatenate([values[:, 1:], following], axis=1)
    gamma = discount[:, None]
    delta = live * (rewards + gamma * keep * live_next * value_next - values)
    decay = gamma * trace[:, None] * keep * live_next
    whole_decay, whole_delta = sent_together((decay, delta), TM, 1, 0)
    _, whole_gain = local_suffix(whole_decay, whole_delta)
    gain = lax.dynamic_slice_in_dim(whole_gain, lax.axis_index(TM) * step_local, step_local, 1)
    returns = live * (gain + values)
    local_count = jnp.sum(live)
    local_total = jnp.sum(gain)
    total, squares, count = (
        one_axis_at_a_time(local_total, DP_TM),
        one_axis_at_a_time(jnp.sum(gain * gain), DP_TM),
        one_axis_at_a_time(local_count, DP_TM),
    )
    mean = total / count
    spread = squares / count - mean * mean
    advantages = live * (gain - mean) / jnp.sqrt(spread + 1e-06)
    return (advantages, returns)


def solution(mesh):
    split = Mesh(mesh.devices.reshape(8, 8, 4, 2), ("dp_0", "dp_1", "tm_0", "tm_1"))
    placed = (
        P(DP, TM, None),
        P(DP, None),
        P(),
        P(),
        P(),
        P(DP, TM),
        P(DP, TM),
        P(DP),
        P(DP),
        P(DP),
    )
    return jax.shard_map(
        on_device, mesh=split, in_specs=placed, out_specs=(P(DP, TM), P(DP, TM)), check_vma=False
    )
```

profile of v0, /device:TPU:1, one launch (start us, length us, event | category | flops | bytes accessed | tf_op | source)
XLA Modules:
  0.0 211.6 jit_solution(15286361352948463845)
XLA Ops:
  7.2 0.7 all-gather.2.cloned.1.call-update
  8.6 0.7 mul.142
  9.2 106.2 %all-gather.2.cloned.1.call-done = bf16[4096,1024]{1,0:T(8,128)(2,1)} async-done(((bf16[64,1024]{1,0:T(8,128)(2,1)}), bf16[4096,1024]{1,0:T(8,128)(2,1)}) %all-gather.2.cloned.1.call-update) | async-done | bytes 8388624 | tf_op jit(solution)/shard_map/all_gather | solution.py:56
  115.4 5.8 %convolution_add_fusion = f32[256,1024]{1,0:T(8,128)S(1)} fusion(bf16[256,4096]{1,0:T(8,128)(2,1)S(1)} %bitcast.24, bf16[4096,1024]{1,0:T(8,128)(2,1)} %all-gather.2.cloned.1.call-done, f32[1024]{0:T(1024)} %param.12), kind=kOutput, calls=%fused_computation | convolution fusion | flops 2147745792 | bytes 11538432 | tf_op jit(solution)/shard_map/dot_general | solution.py:57
  121.2 1.1 fusion
  122.4 2.8 %collective-permute-start = (f32[2,1]{1,0:T(2,128)S(1)}, f32[2,1]{1,0:T(2,128)S(1)}, u32[]{:S(2)}, u32[]{:S(2)}) collective-permute-start(f32[2,1]{1,0:T(2,128)S(1)} %bitcast.35), channel_id=1, source_target_pairs={{1,0},{2,1},{3,2},{4,3},{5,4},{6,5},{7,6},{9,8},{10,9},{11,10},{12... | collective-permute-start | bytes 32 | tf_op jit(solution)/shard_map/ppermute | solution.py:17
  125.2 2.3 %collective-permute-done = f32[2,1]{1,0:T(2,128)S(1)} collective-permute-done((f32[2,1]{1,0:T(2,128)S(1)}, f32[2,1]{1,0:T(2,128)S(1)}, u32[]{:S(2)}, u32[]{:S(2)}) %collective-permute-start) | collective-permute-done | bytes 40 | tf_op jit(solution)/shard_map/ppermute | solution.py:17
  127.6 0.7 compare_select_fusion.4
  128.2 10.8 %all_gather.7 = f32[4,1024]{1,0:T(4,128)S(1)} all-gather(f32[4,128]{1,0:T(4,128)S(1)} %pad_maximum_fusion.1), channel_id=1, replica_groups=mesh['dp_0'=8,'dp_1'=8,'tm_0'=4,'tm_1'=2] {'tm_0','tm_1'}, dimensions={1}, use_global_device_ids=true | all-gather | bytes 18432 | tf_op jit(solution)/shard_map/all_gather | solution.py:22
  139.2 0.2 slice.280
  139.4 0.2 slice.274
  139.6 0.2 slice.270
  139.8 0.2 slice.276
  140.1 0.2 slice.272
  140.3 0.2 slice.267
  140.5 0.4 slice.281
  140.9 0.4 slice.275
  141.3 0.4 slice.277
  141.6 0.4 slice.273
  142.4 0.2 slice.282
  143.1 0.2 slice.279
  148.7 0.4 reverse.8
  149.0 0.4 reverse.7
  152.6 0.3 pad.79
  152.9 0.3 pad.80
  153.2 0.7 rev.2
  153.9 0.6 fusion.15
  154.6 13.8 %all-reduce.21 = (f32[]{:T(128)}, f32[]{:T(128)}, f32[]{:T(128)}) all-reduce(f32[]{:T(128)} %get-tuple-element.3, f32[]{:T(128)} %get-tuple-element.26, f32[]{:T(128)} %get-tuple-element.2), channel_id=1, replica_groups=mesh['dp_0'=8,'dp_1'=8,'tm_0'=4,'tm_1'=2] {'dp_0'}, use_global_device_ids=true, to_apply=%region_11.12 | all-reduce | flops 3 | bytes 24 | tf_op jit(solution)/shard_map/psum | solution.py:30
  168.3 12.5 %all-reduce.20 = (f32[]{:T(128)}, f32[]{:T(128)}, f32[]{:T(128)}) all-reduce(f32[]{:T(128)} %get-tuple-element.7, f32[]{:T(128)} %get-tuple-element.8, f32[]{:T(128)} %get-tuple-element.9), channel_id=1, replica_groups=mesh['dp_0'=8,'dp_1'=8,'tm_0'=4,'tm_1'=2] {'dp_1'}, use_global_device_ids=true, to_apply=%region_12.13 | all-reduce | flops 3 | bytes 24 | tf_op jit(solution)/shard_map/psum | solution.py:30
  180.8 8.2 %all-reduce.22 = (f32[]{:T(128)}, f32[]{:T(128)}, f32[]{:T(128)}) all-reduce(f32[]{:T(128)} %get-tuple-element.4, f32[]{:T(128)} %get-tuple-element.5, f32[]{:T(128)} %get-tuple-element.6), channel_id=1, replica_groups=mesh['dp_0'=8,'dp_1'=8,'tm_0'=4,'tm_1'=2] {'tm_0'}, use_global_device_ids=true, to_apply=%region_13.14 | all-reduce | flops 3 | bytes 24 | tf_op jit(solution)/shard_map/psum | solution.py:30
  189.0 12.4 %all-reduce.23 = (f32[]{:T(128)}, f32[]{:T(128)}, f32[]{:T(128)}) all-reduce(f32[]{:T(128)} %get-tuple-element.10, f32[]{:T(128)} %get-tuple-element.11, f32[]{:T(128)} %get-tuple-element.12), channel_id=1, replica_groups=mesh['dp_0'=8,'dp_1'=8,'tm_0'=4,'tm_1'=2] {'tm_1'}, use_global_device_ids=true, to_apply=%region_14.15 | all-reduce | flops 3 | bytes 24 | tf_op jit(solution)/shard_map/psum | solution.py:30
  204.2 0.6 compare_select_fusion
  (119 shorter events, 9.5 us)
Async XLA Ops:
  7.2 108.2 %copy-start = (bf16[2,128,4096]{2,1,0:T(8,128)(2,1)S(1)}, bf16[2,128,4096]{2,1,0:T(8,128)(2,1)}, u32[]{:S(2)}) copy-start(bf16[2,128,4096]{2,1,0:T(8,128)(2,1)} %param.10) | copy-start | bytes 6291460
  7.2 108.2 %all-gather.2.cloned.1.call-start = ((), (), s32[]{:S(2)}) async-start(), calls=%async_computation | async-start | bytes 8519680 | tf_op jit(solution)/shard_map/all_gather | solution.py:56
  115.4 5.8 %copy-start.5 = (f32[1024]{0:T(1024)S(1)}, f32[1024]{0:T(1024)}, u32[]{:S(2)}) copy-start(f32[1024]{0:T(1024)} %param.13) | copy-start | bytes 12292
  115.4 12.1 %copy-start.1 = (s32[2]{0:T(128)S(1)}, s32[2]{0:T(128)}, u32[]{:S(2)}) copy-start(s32[2]{0:T(128)} %param.17) | copy-start | bytes 28
  115.4 12.1 %copy-start.2 = (s32[2,128]{1,0:T(2,128)S(1)}, s32[2,128]{1,0:T(2,128)}, u32[]{:S(2)}) copy-start(s32[2,128]{1,0:T(2,128)} %param.16) | copy-start | bytes 3076
  115.4 12.1 %copy-start.3 = (f32[2,128]{1,0:T(2,128)S(1)}, f32[2,128]{1,0:T(2,128)}, u32[]{:S(2)}) copy-start(f32[2,128]{1,0:T(2,128)} %param.15) | copy-start | bytes 3076
  115.4 12.1 %copy-start.4 = (f32[2]{0:T(128)S(1)}, f32[2]{0:T(128)}, u32[]{:S(2)}) copy-start(f32[2]{0:T(128)} %param.18) | copy-start | bytes 28
  122.4 5.2 %collective-permute-start = (f32[2,1]{1,0:T(2,128)S(1)}, f32[2,1]{1,0:T(2,128)S(1)}, u32[]{:S(2)}, u32[]{:S(2)}) collective-permute-start(f32[2,1]{1,0:T(2,128)S(1)} %bitcast.35), channel_id=1, source_target_pairs={{1,0},{2,1},{3,2},{4,3},{5,4},{6,5},{7,6},{9,8},{10,9},{11,10},{12... | collective-permute-start | bytes 32 | tf_op jit(solution)/shard_map/ppermute | solution.py:17
Sparse Core Ops, SparseCore 0:
  11.1 104.3 all-gather.1
where the time goes:
time: 212 us
  waiting for transfers between devices  109 us (51%)
  blocking collectives  57.7 us (27%)
  between operations  17.7 us (8%)
  local copies, waits for them, and re-layouts  13.6 us (6%)
  matrix products  6.84 us (3%)
  other arithmetic  3.78 us (2%)
  starting transfers between devices  2.87 us (1%)
    all_gather x1, waiting for transfers between devices, on_device(): whole_weight = lax.all_gather(first_weight, DP, axis=0, tiled=True)  106 us
    psum x4, blocking collectives, one_axis_at_a_time(): return functools.reduce(lax.psum, axes, array)  46.9 us
    all_gather x1, blocking collectives, sent_together(): whole, at, outs = (lax.all_gather(both, axis, axis=dim, tiled=True), 0, [])  10.8 us
    slice x59, local copies, waits for them, and re-layouts, local_suffix(): lax.associative_scan(pair_combine, (decay, delta), reverse=True, axis=1)  9.43 us
    dot_general x1, matrix products, on_device(): pre = jnp.dot(token_rows, whole_weight, preferred_element_type=jnp.float32)  5.75 us
  transfers between devices with their start and end apart: 2, of which 2 were waited for; matrix products, arithmetic and copies ran while one was open for 0% of the time, Pallas kernels for 0%

commit v1 on v0

v1 whole, which is shorter than its diff:
```python
import functools

import jax
import jax.numpy as jnp
from jax import lax
from jax.experimental import pallas as pl
from jax.experimental.pallas import tpu as pltpu
from jax.sharding import Mesh
from jax.sharding import PartitionSpec as P

MESH = pl.DeviceIdType.MESH
DP = ("z", "y")
TM = ("x", "c")


def offsets(n):
    return list(range(-(n // 2 - 1), n // 2 + 1))


def kernel(
    sizes,
    hid, w, b1, w2, rew, don, ln, gm, tr, b2,
    adv, ret,
    H, WA, WB, acc, V, RK, PK, C, GN, G,
    h_loc, w_loc, h_send, h_recv, a_recv, b_recv, w_send,
    rk_send, rk_recv, v_send, v_recv, g_send, g_recv,
):
    NZ, NY, NX = sizes
    NB = NX * 2
    z, y, x, c = (lax.axis_index(a) for a in ("z", "y", "x", "c"))
    (traj, steps), depth = rew.shape, w.shape[0]
    rows = traj * steps
    half = WA.shape[-1]

    def wrap(v, n):
        return lax.rem(v + n, n)

    def remote(src, dst, ss, rs, dev):
        return pltpu.make_async_remote_copy(
            src_ref=src, dst_ref=dst, send_sem=ss, recv_sem=rs, device_id=dev, device_id_type=MESH
        )

    tm_peers = [(i, j) for i in range(NX) for j in range(2) if (i, j) != (0, 0)]
    dp_peers = [(i, j) for i in range(NZ) for j in range(NY) if (i, j) != (0, 0)]

    loads = []
    for p, W in enumerate((WA, WB)):
        cols = pl.ds(pl.multiple_of(c * 2 * half + p * half, half), half)
        loads.append(pltpu.make_async_copy(w.at[:, cols], W.at[z, pl.ds(pl.multiple_of(y * depth, depth), depth)], w_loc.at[p]))
    own_h = H.at[pl.ds(pl.multiple_of(c * rows, rows), rows)]
    loads.append(pltpu.make_async_copy(hid, own_h, h_loc))
    for copy in loads:
        copy.start()

    keep = 1.0 - don[...].astype(jnp.float32)
    RK[x, c, 0:2] = rew[...]
    RK[x, c, 2:4] = keep

    barrier = pltpu.get_barrier_semaphore()
    near = [{"z": wrap(z + 1, NZ)}, {"z": wrap(z - 1, NZ)}, {"y": wrap(y + 1, NY)}, {"y": wrap(y - 1, NY)}]
    far = [{"x": wrap(x + i, NX), "c": wrap(c + j, 2)} for i, j in tm_peers]
    for dev in near + far:
        pl.semaphore_signal(barrier, inc=1, device_id=dev, device_id_type=MESH)
    pl.semaphore_wait(barrier, len(near) + len(far))
    loads[0].wait()
    loads[1].wait()

    oz, oy = offsets(NZ), offsets(NY)
    sends = []
    n_oz, n_oy = len(oz), len(oy)
    sem_of = {(ry, rz): (ry - oy[0]) * n_oz + (rz - oz[0]) for ry in oy for rz in oz}
    zabs = {rz: wrap(z + rz, NZ) for rz in oz}
    yabs = {ry: wrap(y + ry, NY) for ry in oy}

    def place(W, ry, rz):
        return W.at[zabs[rz], pl.ds(pl.multiple_of(yabs[ry] * depth, depth), depth)]

    def hop(part, piece, axis, way):
        ry, rz = piece
        W, sem = (WA, a_recv) if part == 0 else (WB, b_recv)
        n, o = (NZ, rz) if axis == "z" else (NY, ry)
        new = o - way
        if new == -(n // 2):
            new = n // 2
        there = (ry, new) if axis == "z" else (new, rz)
        here = z if axis == "z" else y
        k = len(sends)
        copy = remote(place(W, ry, rz), place(W, ry, rz), w_send.at[k], sem.at[sem_of[there]], {axis: wrap(here + way, n)})
        copy.start()
        sends.append(copy)

    def forwards(part, piece):
        ry, rz = piece
        (ax1, n1, o1), (ax2, n2, o2) = (("z", NZ, rz), ("y", NY, ry)) if part == 0 else (("y", NY, ry), ("z", NZ, rz))
        out = []

        def ahead(n, o, way, last_ok):
            d = abs(o) + 1
            return d < n // 2 or (d == n // 2 and last_ok)

        if o2 == 0:
            for way in (1, -1):
                if o1 == 0 or (o1 < 0) == (way > 0) and abs(o1) < n1 // 2:
                    if ahead(n1, o1, way, way == 1):
                        out.append((ax1, way))
        for way in (1, -1):
            if o2 == 0 or ((o2 < 0) == (way > 0) and abs(o2) < n2 // 2):
                ok = (o1 % 2 == 0) == (way == 1)
                if ahead(n2, o2, way, ok):
                    out.append((ax2, way))
        return out

    for part in (0, 1):
        for axis, way in forwards(part, (0, 0)):
            hop(part, (0, 0), axis, way)

    mate = {"c": 1 - c}
    h_copy = remote(hid, own_h, h_send, h_recv, mate)
    h_copy.start()
    rk_copies = []
    for k, (i, j) in enumerate(tm_peers):
        copy = remote(RK.at[x, c], RK.at[x, c], rk_send.at[k], rk_recv.at[k], far[k])
        copy.start()
        rk_copies.append(copy)

    def tables():
        for copy in rk_copies:
            copy.wait_recv()
        rew16 = jnp.concatenate([RK[b // 2, b % 2, 0:2] for b in range(NB)], axis=0)
        keep16 = jnp.concatenate([RK[b // 2, b % 2, 2:4] for b in range(NB)], axis=0)
        row = lax.broadcasted_iota(jnp.int32, rew16.shape, 0)
        lane = lax.broadcasted_iota(jnp.int32, rew16.shape, 1)
        t = (row // 2) * steps + lane
        odd = row % 2 == 1
        length = jnp.where(odd, ln[1], ln[0])
        gamma = jnp.where(odd, gm[1], gm[0])
        lam = jnp.where(odd, tr[1], tr[0])
        live = (t < length).astype(jnp.float32)
        live_next = (t + 1 < length).astype(jnp.float32)
        C[0] = live
        C[1] = live * rew16
        C[2] = live * gamma * keep16 * live_next
        prod = gamma * lam * keep16 * live_next
        k, span = 0, 1
        while span < NB * steps:
            PK[k] = prod
            prod = prod * shifted(prod, span)
            k, span = k + 1, span * 2

    def shifted(v, span):
        n = NB * 2
        if span >= steps:
            r = 2 * (span // steps)
            return jnp.concatenate([v[r:], v[:r]], axis=0)
        rolled = pltpu.roll(v, steps - span, 1)
        lane = lax.broadcasted_iota(jnp.int32, v.shape, 1)
        return jnp.where(lane < steps - span, rolled, jnp.concatenate([rolled[2:], rolled[:2]], axis=0))

    def matmul(rz, first):
        zz = zabs[rz]
        k = NY * depth
        ks = pl.ds(pl.multiple_of(zz * k, k), k)
        for p, W in enumerate((WA, WB)):
            wv = W[zz]
            for r in range(2):
                rs = pl.ds(r * rows, rows)
                d = jnp.dot(H[rs, ks], wv, preferred_element_type=jnp.float32)
                if first:
                    acc[p, rs] = d
                else:
                    acc[p, rs] += d

    levels = {}
    for ry in oy:
        for rz in oz:
            if (ry, rz) != (0, 0):
                levels.setdefault(abs(ry) + abs(rz), []).append((ry, rz))
    last = max(levels)
    started = False
    for level in range(1, last + 1):
        todo = []
        for ry, rz in levels[level]:
            for part in (0, 1):
                second = ry if part == 0 else rz
                todo.append((abs(second), part, (ry, rz)))
        todo.sort(key=lambda e: (e[0], e[2], e[1]))
        for _, part, piece in todo:
            W, sem = (WA, a_recv) if part == 0 else (WB, b_recv)
            spot = place(W, *piece)
            pltpu.make_async_copy(spot, spot, sem.at[sem_of[piece]]).wait()
            for axis, way in forwards(part, piece):
                hop(part, piece, axis, way)
        if level == 1:
            tables()
        for rz in oz:
            if abs(rz) + NY // 2 == level:
                if not started:
                    loads[2].wait()
                    h_copy.wait_recv()
                matmul(rz, not started)
                started = True

    for r in range(2 * traj):
        rs = pl.ds(r * steps, steps)
        total = jnp.zeros((steps, 128), jnp.float32)
        for p in range(2):
            for q in range(half // 128):
                u = c * (2 * half // 128) + p * (half // 128) + q
                v = acc[p, rs, q * 128:(q + 1) * 128] + b1[pl.ds(u, 1), :]
                total += v / (1.0 + jnp.exp(-v)) * w2[pl.ds(u, 1), :]
        V[c, x, r:r + 1] = jnp.sum(total.T, axis=0, keepdims=True)

    v_copies = []
    for k, (i, j) in enumerate(tm_peers):
        copy = remote(V.at[c, x], V.at[c, x], v_send.at[k], v_recv.at[k], far[k])
        copy.start()
        v_copies.append(copy)
    for copy in sends:
        copy.wait_send()
    h_copy.wait_send()
    for copy in rk_copies:
        copy.wait_send()
    for copy in v_copies:
        copy.wait_recv()

    both = V[0] + V[1]
    v16 = jnp.concatenate([both[b // 2, 2 * (b % 2):2 * (b % 2) + 2] for b in range(NB)], axis=0) + b2[0]
    live = C[0]
    gain = C[1] - live * v16 + C[2] * shifted(v16, 1)
    k, span = 0, 1
    while span < NB * steps:
        gain = gain + PK[k] * shifted(gain, span)
        k, span = k + 1, span * 2

    G[z, y, 0:1] = jnp.sum(gain, axis=0, keepdims=True)
    G[z, y, 1:2] = jnp.sum(gain * gain, axis=0, keepdims=True)
    G[z, y, 2:3] = jnp.sum(live, axis=0, keepdims=True)
    G[z, y, 3:4] = jnp.zeros((1, steps), jnp.float32)
    g_copies = []
    for k, (i, j) in enumerate(dp_peers):
        copy = remote(G.at[z, y], G.at[z, y], g_send.at[k], g_recv.at[k], {"z": wrap(z + i, NZ), "y": wrap(y + j, NY)})
        copy.start()
        g_copies.append(copy)

    back = live * (gain + v16)
    for b in range(NB):
        GN[0, b] = gain[2 * b:2 * b + 2]
        GN[1, b] = back[2 * b:2 * b + 2]
        GN[2, b] = live[2 * b:2 * b + 2]
    me = x * 2 + c
    ret[...] = GN[1, me]
    for copy in v_copies + g_copies:
        copy.wait_send()
    for copy in g_copies:
        copy.wait_recv()
    sums = jnp.sum(jnp.sum(G[...], axis=(0, 1)), axis=1, keepdims=True)
    count = sums[2:3]
    mean = sums[0:1] / count
    spread = sums[1:2] / count - mean * mean
    adv[...] = GN[2, me] * (GN[0, me] - mean) / jnp.sqrt(spread + 1e-06)


def on_device(sizes, hidden, first_weight, first_bias, second_weight, second_bias, rewards, dones, lengths, discount, trace):
    NZ, NY, NX = sizes
    traj, steps, feats = hidden.shape
    depth, units = first_weight.shape
    half = units // 4
    rows = traj * steps
    NB = NX * 2
    vmem = pl.BlockSpec(memory_space=pltpu.VMEM)
    smem = pl.BlockSpec(memory_space=pltpu.SMEM)
    hbm = pl.BlockSpec(memory_space=pl.ANY)
    shape = jax.ShapeDtypeStruct(rewards.shape, jnp.float32)
    dma = pltpu.SemaphoreType.DMA
    n_pieces = NZ * NY
    return pl.pallas_call(
        functools.partial(kernel, sizes),
        out_shape=(shape, shape),
        in_specs=[hbm, hbm, vmem, vmem, vmem, vmem, smem, smem, smem, smem],
        out_specs=(vmem, vmem),
        scratch_shapes=[
            pltpu.VMEM((2 * rows, feats), jnp.bfloat16),
            pltpu.VMEM((NZ, NY * depth, half), jnp.bfloat16),
            pltpu.VMEM((NZ, NY * depth, half), jnp.bfloat16),
            pltpu.VMEM((2, 2 * rows, half), jnp.float32),
            pltpu.VMEM((2, NX, 2 * traj, steps), jnp.float32),
            pltpu.VMEM((NX, 2, 4, steps), jnp.float32),
            pltpu.VMEM((10, 2 * NB, steps), jnp.float32),
            pltpu.VMEM((3, 2 * NB, steps), jnp.float32),
            pltpu.VMEM((3, NB, 2, steps), jnp.float32),
            pltpu.VMEM((NZ, NY, 4, steps), jnp.float32),
            dma, dma((2,)), dma, dma,
            dma((n_pieces,)), dma((n_pieces,)), dma((2 * n_pieces,)),
            dma((NB - 1,)), dma((NB - 1,)), dma((NB - 1,)), dma((NB - 1,)),
            dma((n_pieces - 1,)), dma((n_pieces - 1,)),
        ],
        compiler_params=pltpu.CompilerParams(collective_id=0, has_side_effects=True, vmem_limit_bytes=60 << 20),
    )(
        hidden.reshape(rows, feats), first_weight, first_bias.reshape(-1, 128), second_weight.reshape(-1, 128),
        rewards, dones, lengths, discount, trace, second_bias,
    )


def solution(mesh):
    split = Mesh(mesh.devices.reshape(8, 8, 4, 2), ("z", "y", "x", "c"))
    placed = (
        P(DP, TM, None), P(DP, None), P(), P(), P(), P(DP, TM), P(DP, TM), P(DP), P(DP), P(DP),
    )
    return jax.shard_map(
        functools.partial(on_device, (8, 8, 4)),
        mesh=split, in_specs=placed, out_specs=(P(DP, TM), P(DP, TM)), check_vma=False,
    )
```

time: 212 us -> 65.1 us (0.31)
  waiting for transfers between devices: 109 us -> 0 us
  Pallas kernels: 0 us -> 61.2 us
  blocking collectives: 57.7 us -> 0 us
  between operations: 17.7 us -> 1.29 us
  local copies, waits for them, and re-layouts: 13.6 us -> 2.44 us
  matrix products: 6.84 us -> 0 us
  other arithmetic: 3.78 us -> 0 us
  starting transfers between devices: 2.87 us -> 0 us
    all_gather x1 -> x0, waiting for transfers between devices: 106 us -> none  [on_device(): whole_weight = lax.all_gather(first_weight, DP, axis=0, tiled=True)]
    pallas_call x0 -> x1, Pallas kernels: none -> 61.2 us  [on_device(): pl.pallas_call(functools.partial(kernel, sizes), out_shape=(shape, shape)...]
    psum x4 -> x0, blocking collectives: 46.9 us -> none  [one_axis_at_a_time(): return functools.reduce(lax.psum, axes, array)]
    all_gather x1 -> x0, blocking collectives: 10.8 us -> none  [sent_together(): whole, at, outs = (lax.all_gather(both, axis, axis=dim, tiled=True), 0, [])]
    slice x61 -> x0, local copies, waits for them, and re-layouts: 9.52 us -> none  [the longest x59 9.43 us: local_suffix(): lax.associative_scan(pair_combine, (decay, delta), reverse=True, axis=1)]
    dot_general x2 -> x0, matrix products: 6.84 us -> none  [the longest x1 5.75 us: on_device(): pre = jnp.dot(token_rows, whole_weight, preferred_element_type=jnp.float32)]
    ppermute x1 -> x0, starting transfers between devices: 2.84 us -> none  [passed_along(): return lax.ppermute(block, axis, route)]
    pad x18 -> x0, local copies, waits for them, and re-layouts: 2.59 us -> none  [local_suffix(): lax.associative_scan(pair_combine, (decay, delta), reverse=True, axis=1)]
  transfers between devices with their start and end apart: 2 -> 0, of which waited for: 2 -> 0; matrix products, arithmetic and copies ran while one was open for 0% -> 0% of each run, Pallas kernels for 0% -> 0%
where the time goes in v1:
time: 65.1 us; the launch traced here: 64.9 us
  Pallas kernels  61.2 us (94%)
  local copies, waits for them, and re-layouts  2.44 us (4%)
  between operations  1.29 us (2%)
    pallas_call x1, Pallas kernels, on_device(): pl.pallas_call(functools.partial(kernel, sizes), out_shape=(shape, shape)...  61.2 us
    unnamed x2, local copies, waits for them, and re-layouts  2.44 us

profile of v1, /device:TPU:1, one launch (start us, length us, event | category | flops | bytes accessed | tf_op | source)
XLA Modules:
  0.0 64.9 jit_solution(7935201870371065433)
XLA Ops:
  1.3 61.2 %shard_map.113 = (f32[2,128]{1,0:T(2,128)}, f32[2,128]{1,0:T(2,128)}) custom-call(bf16[256,4096]{1,0:T(8,128)(2,1)} %bitcast.3, bf16[64,1024]{1,0:T(8,128)(2,1)} %w.1, f32[8,128]{1,0:T(8,128)} %bitcast.4, f32[8,128]{1,0:T(8,128)} %bitcast.5, f32[2,128]{1,0:T(2,128)} %rew.1, s32[2,128]{1,0:T(2,128)} %don.1, s32[2]{0:T(128)} %ln.1, f32[2]{0:T(128)} %gm.1, ...), custom_call_target="tpu_custom_call" | custom-call | tf_op jit(solution)/shard_map/pallas_call | solution.py:276
  62.5 1.2 %copy.15 = f32[2,128]{1,0:T(2,128)} copy(f32[2,128]{1,0:T(2,128)} %get-tuple-element.4) | data formatting | bytes 2048
  63.7 1.2 %copy.16 = f32[2,128]{1,0:T(2,128)} copy(f32[2,128]{1,0:T(2,128)} %get-tuple-element.5) | data formatting | bytes 2048

commit v2 on v1

v2 whole, which is shorter than its diff:
```python
import functools

import jax
import jax.numpy as jnp
from jax import lax
from jax.experimental import pallas as pl
from jax.experimental.pallas import tpu as pltpu
from jax.sharding import Mesh
from jax.sharding import PartitionSpec as P

MESH = pl.DeviceIdType.MESH
CHAIN = ((1,), (1,), (1,), (1,))
SKIP = ((1,), (1, 2), (2,), ())
SKIP2 = ((1,), (1,), (1, 2), ())
PAIRS = ((1, 2), (), (1, 2), ())
TABLES_AT = 60
ACROSS_AFTER = 14
HELD = 1
DP = ("z", "y")
TM = ("x", "c")


def offsets(n):
    return list(range(-(n // 2 - 1), n // 2 + 1))


def kernel(
    sizes,
    hid, w, b1, w2, rew, don, ln, gm, tr, b2,
    out,
    H, A, B, X, acc, V, RK, PK, C, GN, G, rewv, donv, b1v, w2v, lns, gms, trs, b2s,
    ld, h_send, h_recv, a_recv, b_recv, w_send, x_send, x_recv,
    rk_send, rk_recv, v_send, v_recv, g_send, g_recv,
):
    NZ, NY, NX = sizes
    NB = NX * 2
    z, y, x, c = (lax.axis_index(a) for a in ("z", "y", "x", "c"))
    (traj, steps), depth = rew.shape, w.shape[0]
    rows = traj * steps
    par = lax.rem(x, 2)
    q, e = depth // 4, depth // 2

    def wrap(v, n):
        return lax.rem(v + n, n)

    def remote(src, dst, ss, rs, dev):
        return pltpu.make_async_remote_copy(
            src_ref=src, dst_ref=dst, send_sem=ss, recv_sem=rs, device_id=dev, device_id_type=MESH
        )

    tm_peers = [(i, j) for i in range(NX) for j in range(2) if (i, j) != (0, 0)]
    dp_peers = [(i, j) for i in range(NZ) for j in range(NY) if (i, j) != (0, 0)]

    loads = []

    def load(src, dst):
        copy = pltpu.make_async_copy(src, dst, ld.at[len(loads)])
        copy.start()
        loads.append(copy)

    def block(j):
        return pl.ds(pl.multiple_of((c * 4 + j) * 128, 128), 128)

    load(rew, rewv)
    load(don, donv)
    own, other = 1 + 2 * par, 3 - 2 * par
    for p, W in enumerate((A, B)):
        load(w.at[p * e:(p + 1) * e, block(0)], W.at[z, y, 0:e])
        load(w.at[p * e:(p + 1) * e, block(own)], W.at[z, y, e:2 * e])
        load(w.at[pl.ds(pl.multiple_of(par * e + p * q, q), q), block(2)], W.at[z, y, 2 * e:2 * e + q])
    n_weights = len(loads)
    own_h = H.at[pl.ds(pl.multiple_of(c * rows, rows), rows)]
    load(hid, own_h)
    for src, dst in ((b1, b1v), (w2, w2v), (ln, lns), (gm, gms), (tr, trs), (b2, b2s)):
        load(src, dst)

    for copy in loads[:2]:
        copy.wait()
    RK[x, c, 0:2] = rewv[...]
    RK[x, c, 2:4] = 1.0 - donv[...].astype(jnp.float32)

    barrier = pltpu.get_barrier_semaphore()
    near = [{"z": wrap(z + d, NZ)} for d in (1, -1, 2, -2)] + [{"y": wrap(y + d, NY)} for d in (1, -1, 2, -2)]
    far = [{"x": wrap(x + i, NX), "c": wrap(c + j, 2)} for i, j in tm_peers]
    for dev in near + far:
        pl.semaphore_signal(barrier, inc=1, device_id=dev, device_id_type=MESH)
    pl.semaphore_wait(barrier, len(near) + len(far))
    for copy in loads[2:n_weights]:
        copy.wait()

    oz, oy = offsets(NZ), offsets(NY)
    sends = []
    n_oz = len(oz)
    sem_of = {(ry, rz): (ry - oy[0]) * n_oz + (rz - oz[0]) for ry in oy for rz in oz}
    zabs = {rz: wrap(z + rz, NZ) for rz in oz}
    yabs = {ry: wrap(y + ry, NY) for ry in oy}

    def place(part, piece):
        ry, rz = piece
        return (A, B)[part].at[zabs[rz], yabs[ry]]

    def norm(o, n):
        return o + n if o < -(n // 2 - 1) else o

    def hop(part, piece, axis, by):
        ry, rz = piece
        sem = (a_recv, b_recv)[part]
        there = (ry, norm(rz - by, NZ)) if axis == "z" else (norm(ry - by, NY), rz)
        here, n = (z, NZ) if axis == "z" else (y, NY)
        spot = place(part, piece)
        copy = remote(spot, spot, w_send.at[len(sends)], sem.at[sem_of[there]], {axis: wrap(here + by, n)})
        copy.start()
        sends.append(copy)

    def across(part, piece):
        ry, rz = piece
        src = place(part, piece).at[e:2 * e + q]
        dst = X.at[zabs[rz], yabs[ry], part * (e + q):(part + 1) * (e + q)]
        by = 1 - 2 * part
        remote(src, dst, x_send, x_recv.at[rz - oz[0]], {"x": wrap(x + by, NX)}).start()

    def forwards(part, piece):
        ry, rz = piece
        (ax1, n1, o1), (ax2, n2, o2) = (("z", NZ, rz), ("y", NY, ry)) if part == 0 else (("y", NY, ry), ("z", NZ, rz))
        first, second = [], []

        def onward(tree, n, o, last):
            out = []
            for way in (1, -1):
                if o == 0 or ((o < 0) == (way > 0) and abs(o) < n // 2):
                    for j in tree[abs(o)]:
                        d = abs(o) + j
                        if d < n // 2 or (d == n // 2 and way == last):
                            out.append(way * j)
            return out

        if o2 == 0:
            first = [(ax1, by) for by in onward(PAIRS, n1, o1, 1)]
        tree = SKIP if abs(o1) >= 3 else CHAIN
        second = [(ax2, by) for by in onward(tree, n2, o2, 1 if o1 % 2 == 0 else -1)]
        return first + second

    for part in (0, 1):
        for axis, by in forwards(part, (0, 0)):
            hop(part, (0, 0), axis, by)
        across(part, (0, 0))

    mate = {"c": 1 - c}
    h_copy = remote(hid, own_h, h_send, h_recv, mate)
    h_copy.start()
    rk_copies = []
    for k, (i, j) in enumerate(tm_peers):
        copy = remote(RK.at[x, c], RK.at[x, c], rk_send.at[k], rk_recv.at[k], far[k])
        copy.start()
        rk_copies.append(copy)

    def tables():
        for copy in rk_copies:
            copy.wait_recv()
        for copy in loads[n_weights + 1:]:
            copy.wait()
        rew16 = jnp.concatenate([RK[b // 2, b % 2, 0:2] for b in range(NB)], axis=0)
        keep16 = jnp.concatenate([RK[b // 2, b % 2, 2:4] for b in range(NB)], axis=0)
        row = lax.broadcasted_iota(jnp.int32, rew16.shape, 0)
        lane = lax.broadcasted_iota(jnp.int32, rew16.shape, 1)
        t = (row // 2) * steps + lane
        odd = row % 2 == 1
        length = jnp.where(odd, lns[1], lns[0])
        gamma = jnp.where(odd, gms[1], gms[0])
        lam = jnp.where(odd, trs[1], trs[0])
        live = (t < length).astype(jnp.float32)
        live_next = (t + 1 < length).astype(jnp.float32)
        C[0] = live
        C[1] = live * rew16
        C[2] = live * gamma * keep16 * live_next
        prod = gamma * lam * keep16 * live_next
        k, span = 0, 1
        while span < NB * steps:
            PK[k] = prod
            prod = prod * shifted(prod, span)
            k, span = k + 1, span * 2

    def shifted(v, span):
        n = NB * 2
        if span >= steps:
            r = 2 * (span // steps)
            return jnp.concatenate([v[r:], v[:r]], axis=0)
        rolled = pltpu.roll(v, steps - span, 1)
        lane = lax.broadcasted_iota(jnp.int32, v.shape, 1)
        return jnp.where(lane < steps - span, rolled, jnp.concatenate([rolled[2:], rolled[:2]], axis=0))

    def hidden_rows(rz, r):
        k = NY * depth
        return H[pl.ds(r * rows, rows), pl.ds(pl.multiple_of(zabs[rz] * k, k), k)]

    def multiply(p, rz, blocks, first):
        wv = jnp.concatenate([jnp.concatenate(b, axis=0) for b in blocks], axis=1)
        for r in range(2):
            rs = pl.ds(r * rows, rows)
            d = jnp.dot(hidden_rows(rz, r), wv, preferred_element_type=jnp.float32)
            if first:
                acc[p, rs] = d
            else:
                acc[p, rs] += d

    def own_part(rz, first):
        zz = zabs[rz]
        block0 = [W[zz, j, 0:e] for j in range(NY) for W in (A, B)]
        mine = [W[zz, j, e:2 * e] for j in range(NY) for W in (A, B)]
        multiply(0, rz, (block0, mine), first)

    def across_part(rz, first):
        zz = zabs[rz]
        pltpu.make_async_copy(X.at[zz], X.at[zz], x_recv.at[rz - oz[0]]).wait()
        theirs, block2 = [], []
        for j in range(NY):
            theirs += [X[zz, j, 0:e], X[zz, j, e + q:2 * e + q]]
            a = jnp.concatenate([A[zz, j, 2 * e:], B[zz, j, 2 * e:]], axis=0)
            b = jnp.concatenate([X[zz, j, e:e + q], X[zz, j, 2 * e + q:]], axis=0)
            block2 += [jnp.where(par == 0, a, b), jnp.where(par == 0, b, a)]
        multiply(1, rz, (theirs, block2), first)

    def passed(part, piece):
        for axis, by in forwards(part, piece):
            hop(part, piece, axis, by)
        across(part, piece)

    def delay(tree, o):
        best = {0: 0.0}
        for d in range(abs(o)):
            for j in tree[d] if d in best else ():
                best[d + j] = best[d] + 1.9 + 0.5 * j
        return best[abs(o)]

    def arrival(part, piece):
        o1, o2 = (piece[1], piece[0]) if part == 0 else piece
        return delay(PAIRS, o1) + delay(SKIP if abs(o1) >= 3 else CHAIN, o2) + 0.1 * abs(o2)

    pieces = [(p, (ry, rz)) for p in (0, 1) for ry in oy for rz in oz if (ry, rz) != (0, 0)]
    pieces.sort(key=lambda e: (arrival(*e), e[1], e[0]))
    events = [(i, 0, p, piece) for i, (p, piece) in enumerate(pieces)]
    for rz in oz:
        done = max(i for i, _, _, piece in events if type(piece) is tuple and piece[1] == rz)
        events.append((done, 1, 0, rz))
        events.append((done + ACROSS_AFTER, 2, 0, rz))
    events.append((TABLES_AT, 3, 0, 0))
    firsts = {1: True, 2: True}
    held = []
    for t, kind, part, what in sorted(events, key=lambda ev: ev[:2]):
        if kind == 0:
            spot = place(part, what)
            pltpu.make_async_copy(spot, spot, (a_recv, b_recv)[part].at[sem_of[what]]).wait()
            if t < HELD:
                held.append((part, what))
                if t == HELD - 1:
                    for one in held:
                        passed(*one)
            else:
                passed(part, what)
        elif kind == 3:
            tables()
        else:
            if kind == 1 and firsts[1]:
                loads[n_weights].wait()
                h_copy.wait_recv()
            (own_part if kind == 1 else across_part)(what, firsts[kind])
            firsts[kind] = False

    for r in range(2 * traj):
        rs = pl.ds(r * steps, steps)
        total = jnp.zeros((steps, 128), jnp.float32)
        for p in range(2):
            for j, u in enumerate(((0, own), (other, 2))[p]):
                u = c * 4 + u
                v = acc[p, rs, j * 128:(j + 1) * 128] + b1v[pl.ds(u, 1), :]
                total += v / (1.0 + jnp.exp(-v)) * w2v[pl.ds(u, 1), :]
        V[c, x, r:r + 1] = jnp.sum(total.T, axis=0, keepdims=True)

    v_copies = []
    for k, (i, j) in enumerate(tm_peers):
        copy = remote(V.at[c, x], V.at[c, x], v_send.at[k], v_recv.at[k], far[k])
        copy.start()
        v_copies.append(copy)
    for copy in sends:
        copy.wait_send()
    pltpu.make_async_copy(X, X, x_send).wait()
    h_copy.wait_send()
    for copy in rk_copies:
        copy.wait_send()
    for copy in v_copies:
        copy.wait_recv()

    both = V[0] + V[1]
    v16 = jnp.concatenate([both[b // 2, 2 * (b % 2):2 * (b % 2) + 2] for b in range(NB)], axis=0) + b2s[0]
    live = C[0]
    gain = C[1] - live * v16 + C[2] * shifted(v16, 1)
    k, span = 0, 1
    while span < NB * steps:
        gain = gain + PK[k] * shifted(gain, span)
        k, span = k + 1, span * 2

    G[z, y, 0:1] = jnp.sum(gain, axis=0, keepdims=True)
    G[z, y, 1:2] = jnp.sum(gain * gain, axis=0, keepdims=True)
    G[z, y, 2:3] = jnp.sum(live, axis=0, keepdims=True)
    G[z, y, 3:4] = jnp.zeros((1, steps), jnp.float32)
    g_copies = []
    for k, (i, j) in enumerate(dp_peers):
        copy = remote(G.at[z, y], G.at[z, y], g_send.at[k], g_recv.at[k], {"z": wrap(z + i, NZ), "y": wrap(y + j, NY)})
        copy.start()
        g_copies.append(copy)

    back = live * (gain + v16)
    for b in range(NB):
        GN[0, b] = gain[2 * b:2 * b + 2]
        GN[1, b] = back[2 * b:2 * b + 2]
        GN[2, b] = live[2 * b:2 * b + 2]
    me = x * 2 + c
    out[1] = GN[1, me]
    for copy in v_copies + g_copies:
        copy.wait_send()
    for copy in g_copies:
        copy.wait_recv()
    sums = jnp.sum(jnp.sum(G[...], axis=(0, 1)), axis=1, keepdims=True)
    count = sums[2:3]
    mean = sums[0:1] / count
    spread = sums[1:2] / count - mean * mean
    out[0] = GN[2, me] * (GN[0, me] - mean) / jnp.sqrt(spread + 1e-06)


def on_device(sizes, hidden, first_weight, first_bias, second_weight, second_bias, rewards, dones, lengths, discount, trace):
    NZ, NY, NX = sizes
    traj, steps, feats = hidden.shape
    depth, units = first_weight.shape
    rows = traj * steps
    NB = NX * 2
    vmem = pl.BlockSpec(memory_space=pltpu.VMEM)
    hbm = pl.BlockSpec(memory_space=pltpu.HBM)
    dma = pltpu.SemaphoreType.DMA
    n_pieces = NZ * NY
    share = depth // 2 + depth // 4
    n_tm = NB - 1
    f32, bf16 = jnp.float32, jnp.bfloat16
    both = pl.pallas_call(
        functools.partial(kernel, sizes),
        out_shape=jax.ShapeDtypeStruct((2, traj, steps), f32),
        in_specs=[hbm] * 10,
        out_specs=vmem,
        scratch_shapes=[
            pltpu.VMEM((2 * rows, feats), bf16),
            pltpu.VMEM((NZ, NY, depth // 2 + share, 128), bf16),
            pltpu.VMEM((NZ, NY, depth // 2 + share, 128), bf16),
            pltpu.VMEM((NZ, NY, 2 * share, 128), bf16),
            pltpu.VMEM((2, 2 * rows, 256), f32),
            pltpu.VMEM((2, NX, 2 * traj, steps), f32),
            pltpu.VMEM((NX, 2, 4, steps), f32),
            pltpu.VMEM((10, 2 * NB, steps), f32),
            pltpu.VMEM((3, 2 * NB, steps), f32),
            pltpu.VMEM((3, NB, 2, steps), f32),
            pltpu.VMEM((NZ, NY, 4, steps), f32),
            pltpu.VMEM((traj, steps), f32),
            pltpu.VMEM((traj, steps), jnp.int32),
            pltpu.VMEM((units // 128, 128), f32),
            pltpu.VMEM((units // 128, 128), f32),
            pltpu.SMEM((traj,), jnp.int32),
            pltpu.SMEM((traj,), f32),
            pltpu.SMEM((traj,), f32),
            pltpu.SMEM((1,), f32),
            dma((15,)), dma, dma,
            dma((n_pieces,)), dma((n_pieces,)), dma((2 * n_pieces,)), dma, dma((NZ,)),
            dma((n_tm,)), dma((n_tm,)), dma((n_tm,)), dma((n_tm,)),
            dma((n_pieces - 1,)), dma((n_pieces - 1,)),
        ],
        compiler_params=pltpu.CompilerParams(collective_id=0, has_side_effects=True, vmem_limit_bytes=60 << 20),
    )(
        hidden.reshape(rows, feats), first_weight, first_bias.reshape(-1, 128), second_weight.reshape(-1, 128),
        rewards, dones, lengths, discount, trace, second_bias,
    )
    return both[0], both[1]


def solution(mesh):
    split = Mesh(mesh.devices.reshape(8, 8, 4, 2), ("z", "y", "x", "c"))
    placed = (
        P(DP, TM, None), P(DP, None), P(), P(), P(), P(DP, TM), P(DP, TM), P(DP), P(DP), P(DP),
    )
    return jax.shard_map(
        functools.partial(on_device, (8, 8, 4)),
        mesh=split, in_specs=placed, out_specs=(P(DP, TM), P(DP, TM)), check_vma=False,
    )
```

time: 65.1 us -> 59.9 us (0.920)
  Pallas kernels: 61.2 us -> 57.1 us
  local copies, waits for them, and re-layouts: 2.44 us -> 1.24 us
    pallas_call x1, Pallas kernels: 61.2 us -> 57.1 us  [on_device(): pl.pallas_call(functools.partial(kernel, sizes), out_shape=jax.ShapeDtype...]
    unnamed x2 -> x0, local copies, waits for them, and re-layouts: 2.44 us -> none
    squeeze x0 -> x1, local copies, waits for them, and re-layouts: none -> 1.24 us  [on_device(): return (both[0], both[1])]
where the time goes in v2:
time: 59.9 us; the launch traced here: 59.6 us
  Pallas kernels  57.1 us (95%)
  between operations  1.29 us (2%)
  local copies, waits for them, and re-layouts  1.24 us (2%)
    pallas_call x1, Pallas kernels, on_device(): pl.pallas_call(functools.partial(kernel, sizes), out_shape=jax.ShapeDtype...  57.1 us
    squeeze x1, local copies, waits for them, and re-layouts, on_device(): return (both[0], both[1])  1.24 us

profile of v2, /device:TPU:1, one launch (start us, length us, event | category | flops | bytes accessed | tf_op | source)
XLA Modules:
  0.0 59.6 jit_solution(12360932209827020271)
XLA Ops:
  1.3 57.1 %shard_map.113 = f32[2,2,128]{2,1,0:T(2,128)} custom-call(bf16[256,4096]{1,0:T(8,128)(2,1)} %bitcast.7, bf16[64,1024]{1,0:T(8,128)(2,1)} %w.1, f32[8,128]{1,0:T(8,128)} %bitcast.8, f32[8,128]{1,0:T(8,128)} %bitcast.9, f32[2,128]{1,0:T(2,128)} %rew.1, s32[2,128]{1,0:T(2,128)} %don.1, s32[2]{0:T(128)} %ln.1, f32[2]{0:T(128)} %gm.1, f32[2]{0:T(128)} %tr.1, ...), custom_call_target="tpu_custom_call" | custom-call | tf_op jit(solution)/shard_map/pallas_call | solution.py:343
  58.4 1.2 %slice_bitcast_fusion = (f32[2,128]{1,0:T(2,128)}, f32[2,128]{1,0:T(2,128)}) fusion(f32[2,2,128]{2,1,0:T(2,128)} %shard_map.113), kind=kLoop, calls=%fused_computation | loop fusion | bytes 4096 | tf_op jit(solution)/shard_map/squeeze | solution.py:378

commit v3 on v2

--- a/solution.py
+++ b/solution.py
@@ -14,7 +14,7 @@
 SKIP2 = ((1,), (1,), (1, 2), ())
 PAIRS = ((1, 2), (), (1, 2), ())
 TABLES_AT = 60
-ACROSS_AFTER = 14
+ACROSS_AFTER = 24
 HELD = 1
 DP = ("z", "y")
 TM = ("x", "c")
@@ -28,8 +28,8 @@
     sizes,
     hid, w, b1, w2, rew, don, ln, gm, tr, b2,
     out,
-    H, A, B, X, acc, V, RK, PK, C, GN, G, rewv, donv, b1v, w2v, lns, gms, trs, b2s,
-    ld, h_send, h_recv, a_recv, b_recv, w_send, x_send, x_recv,
+    H, A, B, X, acc, T, V, RK, PK, C, GN, G, rewv, donv, b1v, w2v, lns, gms, trs, b2s,
+    ld, h_send, h_recv, a_recv, b_recv, a_send, b_send, x_send, x_recv,
     rk_send, rk_recv, v_send, v_recv, g_send, g_recv,
 ):
     NZ, NY, NX = sizes
@@ -53,31 +53,33 @@
 
     loads = []
 
-    def load(src, dst):
-        copy = pltpu.make_async_copy(src, dst, ld.at[len(loads)])
+    def load(src, dst, sem):
+        copy = pltpu.make_async_copy(src, dst, ld.at[sem])
         copy.start()
         loads.append(copy)
 
     def block(j):
         return pl.ds(pl.multiple_of((c * 4 + j) * 128, 128), 128)
 
-    load(rew, rewv)
-    load(don, donv)
+    load(rew, rewv, 2)
+    load(don, donv, 3)
     own, other = 1 + 2 * par, 3 - 2 * par
     for p, W in enumerate((A, B)):
-        load(w.at[p * e:(p + 1) * e, block(0)], W.at[z, y, 0:e])
-        load(w.at[p * e:(p + 1) * e, block(own)], W.at[z, y, e:2 * e])
-        load(w.at[pl.ds(pl.multiple_of(par * e + p * q, q), q), block(2)], W.at[z, y, 2 * e:2 * e + q])
-    n_weights = len(loads)
+        load(w.at[p * e:(p + 1) * e, block(0)], W.at[z * NY + y, 0:e], p)
+        load(w.at[p * e:(p + 1) * e, block(own)], W.at[z * NY + y, e:2 * e], p)
+        load(w.at[pl.ds(pl.multiple_of(par * e + p * q, q), q), block(2)], W.at[z * NY + y, 2 * e:2 * e + q], p)
     own_h = H.at[pl.ds(pl.multiple_of(c * rows, rows), rows)]
-    load(hid, own_h)
-    for src, dst in ((b1, b1v), (w2, w2v), (ln, lns), (gm, gms), (tr, trs), (b2, b2s)):
-        load(src, dst)
+    load(hid, own_h, 4)
+    own_load = loads[-1]
+    for i, (src, dst) in enumerate(((b1, b1v), (w2, w2v), (ln, lns), (gm, gms), (tr, trs), (b2, b2s))):
+        load(src, dst, 5 + i)
+    small_loads = loads[-6:]
 
     for copy in loads[:2]:
         copy.wait()
-    RK[x, c, 0:2] = rewv[...]
-    RK[x, c, 2:4] = 1.0 - donv[...].astype(jnp.float32)
+    me = x * 2 + c
+    RK[me, 0:2] = rewv[...]
+    RK[me, 2:4] = 1.0 - donv[...].astype(jnp.float32)
 
     barrier = pltpu.get_barrier_semaphore()
     near = [{"z": wrap(z + d, NZ)} for d in (1, -1, 2, -2)] + [{"y": wrap(y + d, NY)} for d in (1, -1, 2, -2)]
@@ -85,8 +87,9 @@
     for dev in near + far:
         pl.semaphore_signal(barrier, inc=1, device_id=dev, device_id_type=MESH)
     pl.semaphore_wait(barrier, len(near) + len(far))
-    for copy in loads[2:n_weights]:
-        copy.wait()
+    for p, W in enumerate((A, B)):
+        spot = W.at[z * NY + y]
+        pltpu.make_async_copy(spot, spot, ld.at[p]).wait()
 
     oz, oy = offsets(NZ), offsets(NY)
     sends = []
@@ -97,7 +100,7 @@
 
     def place(part, piece):
         ry, rz = piece
-        return (A, B)[part].at[zabs[rz], yabs[ry]]
+        return (A, B)[part].at[zabs[rz] * NY + yabs[ry]]
 
     def norm(o, n):
         return o + n if o < -(n // 2 - 1) else o
@@ -108,14 +111,14 @@
         there = (ry, norm(rz - by, NZ)) if axis == "z" else (norm(ry - by, NY), rz)
         here, n = (z, NZ) if axis == "z" else (y, NY)
         spot = place(part, piece)
-        copy = remote(spot, spot, w_send.at[len(sends)], sem.at[sem_of[there]], {axis: wrap(here + by, n)})
+        copy = remote(spot, spot, (a_send, b_send)[part], sem.at[sem_of[there]], {axis: wrap(here + by, n)})
         copy.start()
         sends.append(copy)
 
     def across(part, piece):
         ry, rz = piece
         src = place(part, piece).at[e:2 * e + q]
-        dst = X.at[zabs[rz], yabs[ry], part * (e + q):(part + 1) * (e + q)]
+        dst = X.at[zabs[rz] * NY + yabs[ry], part * (e + q):(part + 1) * (e + q)]
         by = 1 - 2 * part
         remote(src, dst, x_send, x_recv.at[rz - oz[0]], {"x": wrap(x + by, NX)}).start()
 
@@ -148,19 +151,19 @@
     mate = {"c": 1 - c}
     h_copy = remote(hid, own_h, h_send, h_recv, mate)
     h_copy.start()
-    rk_copies = []
     for k, (i, j) in enumerate(tm_peers):
-        copy = remote(RK.at[x, c], RK.at[x, c], rk_send.at[k], rk_recv.at[k], far[k])
-        copy.start()
-        rk_copies.append(copy)
+        remote(RK.at[me], RK.at[me], rk_send, rk_recv, far[k]).start()
+
+    def arrived(ref, sem):
+        spots = ref.at[0:ref.shape[0] - 1]
+        pltpu.make_async_copy(spots, spots, sem).wait()
 
     def tables():
-        for copy in rk_copies:
-            copy.wait_recv()
-        for copy in loads[n_weights + 1:]:
+        arrived(RK, rk_recv)
+        for copy in small_loads:
             copy.wait()
-        rew16 = jnp.concatenate([RK[b // 2, b % 2, 0:2] for b in range(NB)], axis=0)
-        keep16 = jnp.concatenate([RK[b // 2, b % 2, 2:4] for b in range(NB)], axis=0)
+        rew16 = jnp.concatenate([RK[b, 0:2] for b in range(NB)], axis=0)
+        keep16 = jnp.concatenate([RK[b, 2:4] for b in range(NB)], axis=0)
         row = lax.broadcasted_iota(jnp.int32, rew16.shape, 0)
         lane = lax.broadcasted_iota(jnp.int32, rew16.shape, 1)
         t = (row // 2) * steps + lane
@@ -205,18 +208,29 @@
 
     def own_part(rz, first):
         zz = zabs[rz]
-        block0 = [W[zz, j, 0:e] for j in range(NY) for W in (A, B)]
-        mine = [W[zz, j, e:2 * e] for j in range(NY) for W in (A, B)]
+        block0 = [W[zz * NY + j, 0:e] for j in range(NY) for W in (A, B)]
+        mine = [W[zz * NY + j, e:2 * e] for j in range(NY) for W in (A, B)]
         multiply(0, rz, (block0, mine), first)
+
+    def projected(p, r):
+        rs = pl.ds(r * steps, steps)
+        total = None
+        for j, u in enumerate(((0, own), (other, 2))[p]):
+            u = c * 4 + u
+            h = 0.5 * (acc[p, rs, j * 128:(j + 1) * 128] + b1v[pl.ds(u, 1), :])
+            term = (h + h * jnp.tanh(h)) * w2v[pl.ds(u, 1), :]
+            total = term if total is None else total + term
+        return total
 
     def across_part(rz, first):
         zz = zabs[rz]
-        pltpu.make_async_copy(X.at[zz], X.at[zz], x_recv.at[rz - oz[0]]).wait()
+        spots = X.at[pl.ds(zz * NY, NY)]
+        pltpu.make_async_copy(spots, spots, x_recv.at[rz - oz[0]]).wait()
         theirs, block2 = [], []
         for j in range(NY):
-            theirs += [X[zz, j, 0:e], X[zz, j, e + q:2 * e + q]]
-            a = jnp.concatenate([A[zz, j, 2 * e:], B[zz, j, 2 * e:]], axis=0)
-            b = jnp.concatenate([X[zz, j, e:e + q], X[zz, j, 2 * e + q:]], axis=0)
+            theirs += [X[zz * NY + j, 0:e], X[zz * NY + j, e + q:2 * e + q]]
+            a = jnp.concatenate([A[zz * NY + j, 2 * e:], B[zz * NY + j, 2 * e:]], axis=0)
+            b = jnp.concatenate([X[zz * NY + j, e:e + q], X[zz * NY + j, 2 * e + q:]], axis=0)
             block2 += [jnp.where(par == 0, a, b), jnp.where(par == 0, b, a)]
         multiply(1, rz, (theirs, block2), first)
 
@@ -246,6 +260,7 @@
     events.append((TABLES_AT, 3, 0, 0))
     firsts = {1: True, 2: True}
     held = []
+    rows_left = NZ
     for t, kind, part, what in sorted(events, key=lambda ev: ev[:2]):
         if kind == 0:
             spot = place(part, what)
@@ -261,37 +276,31 @@
             tables()
         else:
             if kind == 1 and firsts[1]:
-                loads[n_weights].wait()
+                own_load.wait()
                 h_copy.wait_recv()
             (own_part if kind == 1 else across_part)(what, firsts[kind])
             firsts[kind] = False
+            if kind == 1:
+                rows_left -= 1
+                if rows_left == 0:
+                    for r in range(2 * traj):
+                        T[r] = projected(0, r)
 
     for r in range(2 * traj):
-        rs = pl.ds(r * steps, steps)
-        total = jnp.zeros((steps, 128), jnp.float32)
-        for p in range(2):
-            for j, u in enumerate(((0, own), (other, 2))[p]):
-                u = c * 4 + u
-                v = acc[p, rs, j * 128:(j + 1) * 128] + b1v[pl.ds(u, 1), :]
-                total += v / (1.0 + jnp.exp(-v)) * w2v[pl.ds(u, 1), :]
-        V[c, x, r:r + 1] = jnp.sum(total.T, axis=0, keepdims=True)
-
-    v_copies = []
-    for k, (i, j) in enumerate(tm_peers):
-        copy = remote(V.at[c, x], V.at[c, x], v_send.at[k], v_recv.at[k], far[k])
-        copy.start()
-        v_copies.append(copy)
-    for copy in sends:
-        copy.wait_send()
+        V[c * NX + x, r:r + 1] = jnp.sum((T[r] + projected(1, r)).T, axis=0, keepdims=True)
+
+    for dev in far:
+        remote(V.at[c * NX + x], V.at[c * NX + x], v_send, v_recv, dev).start()
+    assert len(sends) == 2 * (NZ * NY - 1)
+    arrived(A, a_send)
+    arrived(B, b_send)
     pltpu.make_async_copy(X, X, x_send).wait()
     h_copy.wait_send()
-    for copy in rk_copies:
-        copy.wait_send()
-    for copy in v_copies:
-        copy.wait_recv()
-
-    both = V[0] + V[1]
-    v16 = jnp.concatenate([both[b // 2, 2 * (b % 2):2 * (b % 2) + 2] for b in range(NB)], axis=0) + b2s[0]
+    arrived(RK, rk_send)
+    arrived(V, v_recv)
+
+    both = V[0:NX] + V[NX:]
+    v16 = jnp.concatenate([both[b // 2, 2 * (b % 2):2 * (b % 2) + 2] for b in range(NB)], axis=0) + b2s[0, 0]
     live = C[0]
     gain = C[1] - live * v16 + C[2] * shifted(v16, 1)
     k, span = 0, 1
@@ -299,28 +308,24 @@
         gain = gain + PK[k] * shifted(gain, span)
         k, span = k + 1, span * 2
 
-    G[z, y, 0:1] = jnp.sum(gain, axis=0, keepdims=True)
-    G[z, y, 1:2] = jnp.sum(gain * gain, axis=0, keepdims=True)
-    G[z, y, 2:3] = jnp.sum(live, axis=0, keepdims=True)
-    G[z, y, 3:4] = jnp.zeros((1, steps), jnp.float32)
-    g_copies = []
-    for k, (i, j) in enumerate(dp_peers):
-        copy = remote(G.at[z, y], G.at[z, y], g_send.at[k], g_recv.at[k], {"z": wrap(z + i, NZ), "y": wrap(y + j, NY)})
-        copy.start()
-        g_copies.append(copy)
+    G[z * NY + y, 0:1] = jnp.sum(gain, axis=0, keepdims=True)
+    G[z * NY + y, 1:2] = jnp.sum(gain * gain, axis=0, keepdims=True)
+    G[z * NY + y, 2:3] = jnp.sum(live, axis=0, keepdims=True)
+    G[z * NY + y, 3:4] = jnp.zeros((1, steps), jnp.float32)
+    for i, j in dp_peers:
+        spot = G.at[z * NY + y]
+        remote(spot, spot, g_send, g_recv, {"z": wrap(z + i, NZ), "y": wrap(y + j, NY)}).start()
 
     back = live * (gain + v16)
     for b in range(NB):
         GN[0, b] = gain[2 * b:2 * b + 2]
         GN[1, b] = back[2 * b:2 * b + 2]
         GN[2, b] = live[2 * b:2 * b + 2]
-    me = x * 2 + c
     out[1] = GN[1, me]
-    for copy in v_copies + g_copies:
-        copy.wait_send()
-    for copy in g_copies:
-        copy.wait_recv()
-    sums = jnp.sum(jnp.sum(G[...], axis=(0, 1)), axis=1, keepdims=True)
+    arrived(V, v_send)
+    arrived(G, g_send)
+    arrived(G, g_recv)
+    sums = jnp.sum(jnp.sum(G[...], axis=0), axis=1, keepdims=True)
     count = sums[2:3]
     mean = sums[0:1] / count
     spread = sums[1:2] / count - mean * mean
@@ -338,7 +343,6 @@
     dma = pltpu.SemaphoreType.DMA
     n_pieces = NZ * NY
     share = depth // 2 + depth // 4
-    n_tm = NB - 1
     f32, bf16 = jnp.float32, jnp.bfloat16
     both = pl.pallas_call(
         functools.partial(kernel, sizes),
@@ -347,16 +351,17 @@
         out_specs=vmem,
         scratch_shapes=[
             pltpu.VMEM((2 * rows, feats), bf16),
-            pltpu.VMEM((NZ, NY, depth // 2 + share, 128), bf16),
-            pltpu.VMEM((NZ, NY, depth // 2 + share, 128), bf16),
-            pltpu.VMEM((NZ, NY, 2 * share, 128), bf16),
+            pltpu.VMEM((NZ * NY, depth // 2 + share, 128), bf16),
+            pltpu.VMEM((NZ * NY, depth // 2 + share, 128), bf16),
+            pltpu.VMEM((NZ * NY, 2 * share, 128), bf16),
             pltpu.VMEM((2, 2 * rows, 256), f32),
-            pltpu.VMEM((2, NX, 2 * traj, steps), f32),
-            pltpu.VMEM((NX, 2, 4, steps), f32),
+            pltpu.VMEM((2 * traj, steps, 128), f32),
+            pltpu.VMEM((NB, 2 * traj, steps), f32),
+            pltpu.VMEM((NB, 4, steps), f32),
             pltpu.VMEM((10, 2 * NB, steps), f32),
             pltpu.VMEM((3, 2 * NB, steps), f32),
             pltpu.VMEM((3, NB, 2, steps), f32),
-            pltpu.VMEM((NZ, NY, 4, steps), f32),
+            pltpu.VMEM((NZ * NY, 4, steps), f32),
             pltpu.VMEM((traj, steps), f32),
             pltpu.VMEM((traj, steps), jnp.int32),
             pltpu.VMEM((units // 128, 128), f32),
@@ -364,16 +369,15 @@
             pltpu.SMEM((traj,), jnp.int32),
             pltpu.SMEM((traj,), f32),
             pltpu.SMEM((traj,), f32),
-            pltpu.SMEM((1,), f32),
-            dma((15,)), dma, dma,
-            dma((n_pieces,)), dma((n_pieces,)), dma((2 * n_pieces,)), dma, dma((NZ,)),
-            dma((n_tm,)), dma((n_tm,)), dma((n_tm,)), dma((n_tm,)),
-            dma((n_pieces - 1,)), dma((n_pieces - 1,)),
+            pltpu.SMEM((1, 1), f32),
+            dma((11,)), dma, dma,
+            dma((n_pieces,)), dma((n_pieces,)), dma, dma, dma, dma((NZ,)),
+            dma, dma, dma, dma, dma, dma,
         ],
         compiler_params=pltpu.CompilerParams(collective_id=0, has_side_effects=True, vmem_limit_bytes=60 << 20),
     )(
         hidden.reshape(rows, feats), first_weight, first_bias.reshape(-1, 128), second_weight.reshape(-1, 128),
-        rewards, dones, lengths, discount, trace, second_bias,
+        rewards, dones, lengths, discount, trace, second_bias.reshape(1, 1),
     )
     return both[0], both[1]
 

time: 59.9 us -> 57.3 us (0.957)
  Pallas kernels: 57.1 us -> 54.6 us
    pallas_call x1, Pallas kernels: 57.1 us -> 54.6 us  [on_device(): pl.pallas_call(functools.partial(kernel, sizes), out_shape=jax.ShapeDtype...]
where the time goes in v3:
time: 57.3 us; the launch traced here: 57.1 us
  Pallas kernels  54.6 us (95%)
  between operations  1.29 us (2%)
  local copies, waits for them, and re-layouts  1.24 us (2%)
    pallas_call x1, Pallas kernels, on_device(): pl.pallas_call(functools.partial(kernel, sizes), out_shape=jax.ShapeDtype...  54.6 us
    squeeze x1, local copies, waits for them, and re-layouts, on_device(): return (both[0], both[1])  1.24 us

profile of v3, /device:TPU:1, one launch (start us, length us, event | category | flops | bytes accessed | tf_op | source)
XLA Modules:
  0.0 57.1 jit_solution(7819103907484014850)
XLA Ops:
  1.3 54.6 %shard_map.113 = f32[2,2,128]{2,1,0:T(2,128)} custom-call(bf16[256,4096]{1,0:T(8,128)(2,1)} %bitcast.9, bf16[64,1024]{1,0:T(8,128)(2,1)} %w.1, f32[8,128]{1,0:T(8,128)} %bitcast.10, f32[8,128]{1,0:T(8,128)} %bitcast.11, f32[2,128]{1,0:T(2,128)} %rew.1, s32[2,128]{1,0:T(2,128)} %don.1, s32[2]{0:T(128)} %ln.1, f32[2]{0:T(128)} %gm.1, f32[2]{0:T(128)} %tr.1, ...), custom_call_target="tpu_custom_call" | custom-call | tf_op jit(solution)/shard_map/pallas_call | solution.py:347
  55.9 1.2 %slice_bitcast_fusion = (f32[2,128]{1,0:T(2,128)}, f32[2,128]{1,0:T(2,128)}) fusion(f32[2,2,128]{2,1,0:T(2,128)} %shard_map.113), kind=kLoop, calls=%fused_computation | loop fusion | bytes 4096 | tf_op jit(solution)/shard_map/squeeze | solution.py:382

commit v4 on v3

--- a/solution.py
+++ b/solution.py
@@ -13,7 +13,7 @@
 SKIP = ((1,), (1, 2), (2,), ())
 SKIP2 = ((1,), (1,), (1, 2), ())
 PAIRS = ((1, 2), (), (1, 2), ())
-TABLES_AT = 60
+TABLES_AT = 11.5
 ACROSS_AFTER = 24
 HELD = 1
 DP = ("z", "y")
@@ -139,7 +139,7 @@
 
         if o2 == 0:
             first = [(ax1, by) for by in onward(PAIRS, n1, o1, 1)]
-        tree = SKIP if abs(o1) >= 3 else CHAIN
+        tree = SKIP if abs(o1) >= 4 else CHAIN
         second = [(ax2, by) for by in onward(tree, n2, o2, 1 if o1 % 2 == 0 else -1)]
         return first + second
 
@@ -248,7 +248,7 @@
 
     def arrival(part, piece):
         o1, o2 = (piece[1], piece[0]) if part == 0 else piece
-        return delay(PAIRS, o1) + delay(SKIP if abs(o1) >= 3 else CHAIN, o2) + 0.1 * abs(o2)
+        return delay(PAIRS, o1) + delay(SKIP if abs(o1) >= 4 else CHAIN, o2) + 0.6 * abs(o2)
 
     pieces = [(p, (ry, rz)) for p in (0, 1) for ry in oy for rz in oz if (ry, rz) != (0, 0)]
     pieces.sort(key=lambda e: (arrival(*e), e[1], e[0]))

time: 57.3 us -> 56.8 us (level)
  no operation moved by 1% of the time
where the time goes in v4:
time: 56.8 us; the launch traced here: 56.6 us
  Pallas kernels  54.1 us (95%)
  between operations  1.29 us (2%)
  local copies, waits for them, and re-layouts  1.24 us (2%)
    pallas_call x1, Pallas kernels, on_device(): pl.pallas_call(functools.partial(kernel, sizes), out_shape=jax.ShapeDtype...  54.1 us
    squeeze x1, local copies, waits for them, and re-layouts, on_device(): return (both[0], both[1])  1.24 us

profile of v4, /device:TPU:1, one launch (start us, length us, event | category | flops | bytes accessed | tf_op | source)
XLA Modules:
  0.0 56.6 jit_solution(3945176515073086771)
XLA Ops:
  1.3 54.1 %shard_map.113 = f32[2,2,128]{2,1,0:T(2,128)} custom-call(bf16[256,4096]{1,0:T(8,128)(2,1)} %bitcast.9, bf16[64,1024]{1,0:T(8,128)(2,1)} %w.1, f32[8,128]{1,0:T(8,128)} %bitcast.10, f32[8,128]{1,0:T(8,128)} %bitcast.11, f32[2,128]{1,0:T(2,128)} %rew.1, s32[2,128]{1,0:T(2,128)} %don.1, s32[2]{0:T(128)} %ln.1, f32[2]{0:T(128)} %gm.1, f32[2]{0:T(128)} %tr.1, ...), custom_call_target="tpu_custom_call" | custom-call | tf_op jit(solution)/shard_map/pallas_call | solution.py:347
  55.4 1.2 %slice_bitcast_fusion = (f32[2,128]{1,0:T(2,128)}, f32[2,128]{1,0:T(2,128)}) fusion(f32[2,2,128]{2,1,0:T(2,128)} %shard_map.113), kind=kLoop, calls=%fused_computation | loop fusion | bytes 4096 | tf_op jit(solution)/shard_map/squeeze | solution.py:382
